TPU v7x, 256 devices: a whole 4x4x8 slice. The times are simulated.
256 devices in a mesh: dp: 32 (over x, z), seq: 8 (over y, core).
Axes of the slice: x: 4, y: 4, z: 8, core: 2. Of those that a mesh axis runs over, the one named last changes fastest.
Arguments:
- hidden: bfloat16 [32, 8192, 4096], P('dp', 'seq'), may hold values from -6 to 6
- value_weight: bfloat16 [4096, 64], replicated, may hold values from -0.09375 to 0.09375
- value_bias: float32 [64], replicated, may hold values from -1 to 1
- returns: float32 [32, 8192], P('dp', 'seq'), may hold values from -12 to 12, as said below
- task_bins: int32 [32, 8192], P('dp', 'seq'), may hold values from 0 to 63
- loss_mask: int32 [32, 8192], P('dp', 'seq'), may hold values 0 or 1
Outputs:
- targets: float32 [32, 8192], P('dp', 'seq')
- weight_grad: float32 [4096, 64], replicated
- bias_grad: float32 [64], replicated
Inputs may be any that keep to these rules, and one draw needn't show every extreme that they name: The returns of one rollout share a level and a trend along positions.
All inputs are finite; a program needn't handle non-finite values.
Results may differ from a plain program's by a relative error of at most 0.00083.
Values sent between devices are 32-bit elements.
A program may use at most 64 MiB of HBM per device.

v0:
```python
import jax
import jax.numpy as jnp
from jax import lax
from jax.sharding import Mesh
from jax.sharding import PartitionSpec as P

DP = ("dp_0", "dp_1")
DP_SEQ = ("dp_0", "dp_1", "seq_0", "seq_1")
SEQ = ("seq_0", "seq_1")


def one_axis_at_a_time(x, axes):
    for axis in axes:
        x = lax.psum(x, axis)
    return x


def in_blocks(x, dim, devices):
    shape = x.shape
    pieces = x.reshape(*shape[:dim], devices, shape[dim] // devices, *shape[dim + 1 :])
    return jnp.moveaxis(pieces, dim, 0)


def sent_and_summed(x, axis, dim):
    devices = lax.axis_size(axis)
    pieces = lax.all_to_all(in_blocks(x, dim, devices), axis, 0, 0, tiled=True)
    return jnp.sum(pieces, axis=0)


def over_pieces(x, axis):
    pieces = lax.all_gather(x, axis)
    return pieces.sum(axis=0)


def in_order(pieces, dim):
    pieces = jnp.moveaxis(pieces, 0, dim)
    shape = pieces.shape
    return pieces.reshape(*shape[:dim], shape[dim] * shape[dim + 1], *shape[dim + 2 :])


def one_gather(arrays, axis, dims):
    ravelled = jnp.concatenate([a.reshape(-1) for a in arrays])
    lines, at, outs = (lax.all_gather(ravelled, axis), 0, [])
    for a, dim in zip(arrays, dims):
        pieces = lines[:, at : at + a.size].reshape(-1, *a.shape)
        outs.append(in_order(pieces, dim))
        at += a.size
    return tuple(outs)


def on_device(hidden, value_weight, value_bias, returns, task_bins, loss_mask):
    rollouts = hidden.shape[0] * lax.axis_size(DP)
    states = hidden.reshape(-1, hidden.shape[2])
    flat_returns = returns.reshape(-1)
    bins_iota = jnp.arange(value_weight.shape[1], dtype=jnp.int32)
    chosen = (task_bins.reshape(-1)[:, None] == bins_iota).astype(jnp.float32)
    valid = loss_mask.reshape(-1).astype(jnp.float32)
    onehot = chosen * valid[:, None]
    scores = jnp.dot(states, value_weight, preferred_element_type=jnp.float32)
    counts = jnp.sum(onehot, axis=0)
    summed = jnp.sum(onehot * flat_returns[:, None], axis=0)
    squares = jnp.sum(onehot * flat_returns[:, None] * flat_returns[:, None], axis=0)
    counts, summed, squares = (
        one_axis_at_a_time(counts, DP_SEQ),
        one_axis_at_a_time(summed, DP_SEQ),
        one_axis_at_a_time(squares, DP_SEQ),
    )
    means = summed / jnp.maximum(counts, 1.0)
    second = squares - summed * means
    floor_counts = jnp.maximum(counts, 1.0)
    spread = jnp.sqrt(second / floor_counts + 0.1)
    deviation = flat_returns[:, None] - means
    targets = jnp.sum(chosen * (deviation / spread), axis=-1)
    predicted = jnp.sum((scores + value_bias) * chosen, axis=-1)
    slope = valid * jnp.clip(predicted - targets, -1.0, 1.0) / rollouts
    coefficient = chosen * slope[:, None]
    weight_grad = lax.dot_general(
        states,
        coefficient.astype(jnp.bfloat16),
        (((0,), (0,)), ((), ())),
        preferred_element_type=jnp.float32,
    )
    bias_grad = jnp.sum(coefficient, axis=0)
    weight_share, bias_share = (
        sent_and_summed(weight_grad, SEQ, 0),
        sent_and_summed(bias_grad, SEQ, 0),
    )
    weight_share, bias_share = (over_pieces(weight_share, DP), over_pieces(bias_share, DP))
    weight_grad, bias_grad = one_gather((weight_share, bias_share), SEQ, (0, 0))
    return (targets.reshape(returns.shape), weight_grad, bias_grad)


def solution(mesh):
    torus = Mesh(mesh.devices.reshape(4, 8, 4, 2), ("dp_0", "dp_1", "seq_0", "seq_1"))
    return jax.shard_map(
        on_device,
        mesh=torus,
        in_specs=(P(DP, SEQ, None), P(), P(), P(DP, SEQ), P(DP, SEQ), P(DP, SEQ)),
        out_specs=(P(DP, SEQ), P(), P()),
        check_vma=False,
    )
```

profile of v0, /device:TPU:2, one launch (start us, length us, event | category | flops | bytes accessed | tf_op | source)
XLA Modules:
  0.0 242.7 jit_solution(15174251492240911007)
XLA Ops:
  7.2 0.7 convert_element_type.17
  8.0 0.9 fusion.14
  8.9 10.0 %all-reduce.4 = (f32[64]{0:T(128)S(1)}, f32[64]{0:T(128)S(1)}, f32[64]{0:T(128)S(1)}) all-reduce(f32[64]{0:T(128)S(1)} %get-tuple-element.13, f32[64]{0:T(128)S(1)} %get-tuple-element.12, f32[64]{0:T(128)S(1)} %get-tuple-element.14), channel_id=1, replica_groups=mesh['dp_0'=4,'dp_1'=8,'seq_0'=4,'seq_1'=2] {'dp_0'}, use_global_device_ids=true, to_apply=%region_11.0 | all-reduce | flops 192 | bytes 1536 | tf_op jit(solution)/shard_map/psum | solution.py:14
  18.8 18.6 %all-reduce.2 = (f32[64]{0:T(128)S(1)}, f32[64]{0:T(128)S(1)}, f32[64]{0:T(128)S(1)}) all-reduce(f32[64]{0:T(128)S(1)} %get-tuple-element.21, f32[64]{0:T(128)S(1)} %get-tuple-element.22, f32[64]{0:T(128)S(1)} %get-tuple-element.23), channel_id=1, replica_groups=mesh['dp_0'=4,'dp_1'=8,'seq_0'=4,'seq_1'=2] {'dp_1'}, use_global_device_ids=true, to_apply=%region_12.0 | all-reduce | flops 192 | bytes 1536 | tf_op jit(solution)/shard_map/psum | solution.py:14
  37.5 10.7 %all-reduce.3 = (f32[64]{0:T(128)S(1)}, f32[64]{0:T(128)S(1)}, f32[64]{0:T(128)S(1)}) all-reduce(f32[64]{0:T(128)S(1)} %get-tuple-element.15, f32[64]{0:T(128)S(1)} %get-tuple-element.16, f32[64]{0:T(128)S(1)} %get-tuple-element.17), channel_id=1, replica_groups=mesh['dp_0'=4,'dp_1'=8,'seq_0'=4,'seq_1'=2] {'seq_0'}, use_global_device_ids=true, to_apply=%region_13.0 | all-reduce | flops 192 | bytes 1536 | tf_op jit(solution)/shard_map/psum | solution.py:14
  48.2 2.5 %all-reduce.5 = (f32[64]{0:T(128)S(1)}, f32[64]{0:T(128)S(1)}, f32[64]{0:T(128)S(1)}) all-reduce(f32[64]{0:T(128)S(1)} %get-tuple-element.18, f32[64]{0:T(128)S(1)} %get-tuple-element.19, f32[64]{0:T(128)S(1)} %get-tuple-element.20), channel_id=1, replica_groups=mesh['dp_0'=4,'dp_1'=8,'seq_0'=4,'seq_1'=2] {'seq_1'}, use_global_device_ids=true, to_apply=%region_14.0 | all-reduce | flops 192 | bytes 1536 | tf_op jit(solution)/shard_map/psum | solution.py:14
  50.7 0.8 select_reduce_fusion.2
  51.6 6.2 %fusion.10 = f32[1024]{0:T(1024)S(1)} fusion(bf16[4096,64]{0,1:T(8,128)(2,1)S(1)} %copy-done, bf16[1,1024,4096]{2,1,0:T(8,128)(2,1)} %param.6, f32[64]{0:T(128)} %param.8, s32[1024]{0:T(1024)} %bitcast.34), kind=kOutput, calls=%fused_computation.7 | convolution fusion | flops 537132032 | bytes 8921344 | tf_op jit(solution)/shard_map/dot_general | solution.py:59
  57.9 1.6 fusion
  59.5 18.4 %all_to_all.14 = f32[8,512,64]{1,2,0:T(8,128)S(1)} all-to-all(f32[8,512,64]{1,2,0:T(8,128)S(1)} %bitcast.30), channel_id=1, replica_groups=mesh['dp_0'=4,'dp_1'=8,'seq_0'=4,'seq_1'=2] {'seq_0','seq_1'}, dimensions={0} | all-to-all | bytes 2097152 | tf_op jit(solution)/shard_map/all_to_all | solution.py:26
  77.9 0.7 reduce_sum.95
  78.7 0.1 select_reduce_fusion
  78.8 0.7 all_to_all.10
  79.5 3.3 %all-to-all-start.1 = ((f32[8,1,8]{2,1,0:T(1,128)}), f32[8,1,8]{2,1,0:T(1,128)S(1)}, u32[]{:S(2)}, u32[]{:S(2)}) async-start(f32[8,1,8]{2,1,0:T(1,128)} %bitcast.6), calls=%async_computation.1 | async-start | bytes 8192 | tf_op jit(solution)/shard_map/all_to_all | solution.py:26
  82.8 0.6 dynamic-slice.1
  83.4 0.6 dynamic-slice
  85.3 2.7 %all-to-all-done.1 = f32[8,1,8]{2,1,0:T(1,128)S(1)} async-done(((f32[8,1,8]{2,1,0:T(1,128)}), f32[8,1,8]{2,1,0:T(1,128)S(1)}, u32[]{:S(2)}, u32[]{:S(2)}) %all-to-all-start.1) | async-done | bytes 288 | tf_op jit(solution)/shard_map/all_to_all | solution.py:26
  88.0 0.2 dynamic-update-slice
  88.2 62.2 %all-reduce = f32[256]{0:T(256)S(1)} all-reduce(f32[256]{0:T(256)S(1)} %dynamic-update-slice), channel_id=3, replica_groups=mesh['dp_0'=4,'dp_1'=8,'seq_0'=4,'seq_1'=2] {'dp_0','dp_1'}, use_global_device_ids=true, to_apply=%add | all-reduce | flops 256 | bytes 2048
  150.5 4.8 %all-gather.5.cloned.1.call-done = f32[16384,64]{0,1:T(8,128)} async-done(((f32[512,64]{0,1:T(8,128)}), f32[16384,64]{0,1:T(8,128)}) %all-gather.5.cloned.1.call-update) | async-done | bytes 4194320 | tf_op jit(solution)/shard_map/all_gather | solution.py:31
  155.4 4.6 %copy.21 = f32[8,8,32,512]{3,2,1,0:T(8,128)S(1)} copy(f32[8,8,32,512]{3,1,2,0:T(8,128)} %bitcast.29) | data formatting | bytes 8388608
  159.9 0.7 bitcast_reduce_fusion
  160.6 0.1 copy.16
  160.7 0.1 reshape.51
  160.9 0.5 maximum_dynamic-update-slice_fusion
  161.5 1.0 copy-done.2
  162.5 66.3 %all-reduce.8.cloned.1.call-done = f32[262208]{0:T(1024)} async-done(((f32[262208]{0:T(1024)}), f32[262208]{0:T(1024)}) %all-reduce.8.cloned.1.call-update) | async-done | bytes 1048848
  228.8 1.8 reshape.55
  230.6 1.0 slice.8
  231.6 0.6 reshape.52
  232.2 2.1 reshape_reshape.3
  234.3 1.6 copy.18
  (26 shorter events, 0.5 us)
Async XLA Ops:
  7.2 44.4 %copy-start = (bf16[4096,64]{0,1:T(8,128)(2,1)S(1)}, bf16[4096,64]{0,1:T(8,128)(2,1)}, u32[]{:S(2)}) copy-start(bf16[4096,64]{0,1:T(8,128)(2,1)} %param.7) | copy-start | bytes 1572868
  7.2 148.2 %all-gather.5.cloned.1.call-start = ((), (), s32[]{:S(2)}) async-start(), calls=%async_computation.2 | async-start | bytes 4325376 | tf_op jit(solution)/shard_map/all_gather | solution.py:31
  51.5 6.3 %copy-start.4 = (f32[1024]{0:T(1024)}, f32[1024]{0:T(1024)S(1)}, u32[]{:S(2)}) copy-start(f32[1024]{0:T(1024)S(1)} %select_reduce_fusion.2) | copy-start | bytes 12292
  51.6 6.3 %copy-start.1 = (bf16[1,1024,4096]{2,1,0:T(8,128)(2,1)S(1)}, bf16[1,1024,4096]{2,1,0:T(8,128)(2,1)}, u32[]{:S(2)}) copy-start(bf16[1,1024,4096]{2,1,0:T(8,128)(2,1)} %param.6) | copy-start | bytes 25165828
  51.6 6.3 %copy-start.3 = (s32[1,1024]{1,0:T(1,128)S(1)}, s32[1,1024]{1,0:T(1,128)}, u32[]{:S(2)}) copy-start(s32[1,1024]{1,0:T(1,128)} %param.10) | copy-start | bytes 12292
  59.4 23.4 %copy-start.6 = (u32[256]{0:T(256)S(1)}, u32[256]{0:T(256)}, u32[]{:S(2)}) copy-start(u32[256]{0:T(256)} %constant.27) | copy-start | bytes 3076
  59.4 24.0 %copy-start.5 = (u32[256]{0:T(256)S(1)}, u32[256]{0:T(256)}, u32[]{:S(2)}) copy-start(u32[256]{0:T(256)} %constant.22) | copy-start | bytes 3076
  79.5 8.5 %all-to-all-start.1 = ((f32[8,1,8]{2,1,0:T(1,128)}), f32[8,1,8]{2,1,0:T(1,128)S(1)}, u32[]{:S(2)}, u32[]{:S(2)}) async-start(f32[8,1,8]{2,1,0:T(1,128)} %bitcast.6), calls=%async_computation.1 | async-start | bytes 8192 | tf_op jit(solution)/shard_map/all_to_all | solution.py:26
  82.8 146.0 %all-reduce.8.cloned.1.call-start = ((), (), s32[]{:S(2)}) async-start(), calls=%async_computation.3 | async-start | bytes 2105344
  161.4 1.0 copy-start.2
Sparse Core Ops, SparseCore 0:
  78.8 76.5 all-gather.4
  162.6 66.0 all-reduce.7
where the time goes:
time: 243 us
  blocking collectives  122 us (50%)
  waiting for transfers between devices  73.8 us (30%)
  between operations  15.5 us (6%)
  local copies, waits for them, and re-layouts  15.2 us (6%)
  matrix products  7.79 us (3%)
  other arithmetic  4.6 us (2%)
  starting transfers between devices  3.34 us (1%)
    unnamed x3, waiting for transfers between devices  66.3 us
    unnamed x1, blocking collectives  62.2 us
    psum x4, blocking collectives, one_axis_at_a_time(): x = lax.psum(x, axis)  41.8 us
    all_to_all x1, blocking collectives, sent_and_summed(): pieces = lax.all_to_all(in_blocks(x, dim, devices), axis, 0, 0, tiled=True)  18.4 us
    unnamed x21, local copies, waits for them, and re-layouts  8.7 us
    dot_general x1, matrix products, on_device(): scores = jnp.dot(states, value_weight, preferred_element_type=jnp.float32)  6.22 us
  transfers between devices with their start and end apart: 3, of which 3 were waited for; matrix products, arithmetic and copies ran while one was open for 1% of the time, Pallas kernels for 0%

commit v1 on v0

--- a/solution.py
+++ b/solution.py
@@ -11,7 +11,8 @@
 
 def one_axis_at_a_time(x, axes):
     for axis in axes:
-        x = lax.psum(x, axis)
+        parts = lax.all_gather(x, axis, axis=0, tiled=False)
+        x = parts.sum(axis=0)
     return x
 
 

time: 243 us -> 255 us (1.049)
  local copies, waits for them, and re-layouts: 15.2 us -> 24 us
  between operations: 15.5 us -> 18.2 us
    unnamed x1 -> x5, blocking collectives: 62.2 us -> 104 us
    psum x4 -> x0, blocking collectives: 41.8 us -> none  [one_axis_at_a_time(): x = lax.psum(x, axis)]
    unnamed x21 -> x49, local copies, waits for them, and re-layouts: 8.7 us -> 16.5 us
where the time goes in v1:
time: 255 us; the launch traced here: 254 us
  blocking collectives  123 us (48%)
  waiting for transfers between devices  73.8 us (29%)
  local copies, waits for them, and re-layouts  24 us (9%)
  between operations  18.2 us (7%)
  matrix products  7.78 us (3%)
  other arithmetic  4.78 us (2%)
  starting transfers between devices  3.34 us (1%)
    unnamed x5, blocking collectives  104 us
    unnamed x3, waiting for transfers between devices  66.3 us
    all_to_all x1, blocking collectives, sent_and_summed(): pieces = lax.all_to_all(in_blocks(x, dim, devices), axis, 0, 0, tiled=True)  18.4 us
    unnamed x49, local copies, waits for them, and re-layouts  16.5 us
    dot_general x1, matrix products, on_device(): scores = jnp.dot(states, value_weight, preferred_element_type=jnp.float32)  6.22 us
  transfers between devices with their start and end apart: 3, of which 3 were waited for; matrix products, arithmetic and copies ran while one was open for 1% of the time, Pallas kernels for 0%

profile of v1, /device:TPU:2, one launch (start us, length us, event | category | flops | bytes accessed | tf_op | source)
XLA Modules:
  0.0 254.5 jit_solution(10965668891434443050)
XLA Ops:
  7.2 1.3 dynamic-slice.3
  8.5 1.3 dynamic-slice.2
  11.1 1.3 dynamic-slice.1
  13.0 1.3 dynamic-slice
  14.9 0.7 convert_element_type.17
  15.6 0.9 fusion.14
  17.2 9.9 %all-reduce.16 = (f32[256]{0:T(256)S(1)}, f32[256]{0:T(256)S(1)}, f32[256]{0:T(256)S(1)}) all-reduce(f32[256]{0:T(256)S(1)} %dynamic-update-slice.8, f32[256]{0:T(256)S(1)} %dynamic-update-slice, f32[256]{0:T(256)S(1)} %dynamic-update-slice.4), channel_id=10, replica_groups=mesh['dp_0'=4,'dp_1'=8,'seq_0'=4,'seq_1'=2] {'dp_0'}, use_global_device_ids=true, to_apply=%add.8 | all-reduce | flops 768 | bytes 6144
  28.1 18.9 %all-reduce.14 = (f32[512]{0:T(512)S(1)}, f32[512]{0:T(512)S(1)}, f32[512]{0:T(512)S(1)}) all-reduce(f32[512]{0:T(512)S(1)} %dynamic-update-slice.9, f32[512]{0:T(512)S(1)} %dynamic-update-slice.1, f32[512]{0:T(512)S(1)} %dynamic-update-slice.5), channel_id=11, replica_groups=mesh['dp_0'=4,'dp_1'=8,'seq_0'=4,'seq_1'=2] {'dp_1'}, use_global_device_ids=true, to_apply=%add.9 | all-reduce | flops 1536 | bytes 12288
  48.0 10.7 %all-reduce.15 = (f32[256]{0:T(256)S(1)}, f32[256]{0:T(256)S(1)}, f32[256]{0:T(256)S(1)}) all-reduce(f32[256]{0:T(256)S(1)} %dynamic-update-slice.10, f32[256]{0:T(256)S(1)} %dynamic-update-slice.2, f32[256]{0:T(256)S(1)} %dynamic-update-slice.6), channel_id=12, replica_groups=mesh['dp_0'=4,'dp_1'=8,'seq_0'=4,'seq_1'=2] {'seq_0'}, use_global_device_ids=true, to_apply=%add.10 | all-reduce | flops 768 | bytes 6144
  59.7 2.4 all-reduce.17
  62.5 0.8 select_reduce_fusion.2
  63.4 6.2 %fusion.10 = f32[1024]{0:T(1024)S(1)} fusion(bf16[4096,64]{0,1:T(8,128)(2,1)S(1)} %copy-done, bf16[1,1024,4096]{2,1,0:T(8,128)(2,1)} %param.6, f32[64]{0:T(128)} %param.8, s32[1024]{0:T(1024)} %bitcast.38), kind=kOutput, calls=%fused_computation.7 | convolution fusion | flops 537132032 | bytes 8921344 | tf_op jit(solution)/shard_map/dot_general | solution.py:60
  69.6 1.6 fusion
  71.3 18.4 %all_to_all.14 = f32[8,512,64]{1,2,0:T(8,128)S(1)} all-to-all(f32[8,512,64]{1,2,0:T(8,128)S(1)} %bitcast.34), channel_id=1, replica_groups=mesh['dp_0'=4,'dp_1'=8,'seq_0'=4,'seq_1'=2] {'seq_0','seq_1'}, dimensions={0} | all-to-all | bytes 2097152 | tf_op jit(solution)/shard_map/all_to_all | solution.py:27
  89.7 0.7 reduce_sum.215
  90.6 0.7 all_to_all.10
  91.3 3.3 %all-to-all-start.1 = ((f32[8,1,8]{2,1,0:T(1,128)}), f32[8,1,8]{2,1,0:T(1,128)S(1)}, u32[]{:S(2)}, u32[]{:S(2)}) async-start(f32[8,1,8]{2,1,0:T(1,128)} %bitcast.10), calls=%async_computation.1 | async-start | bytes 8192 | tf_op jit(solution)/shard_map/all_to_all | solution.py:27
  94.6 0.6 dynamic-slice.13
  95.2 0.6 dynamic-slice.12
  97.1 2.7 %all-to-all-done.1 = f32[8,1,8]{2,1,0:T(1,128)S(1)} async-done(((f32[8,1,8]{2,1,0:T(1,128)}), f32[8,1,8]{2,1,0:T(1,128)S(1)}, u32[]{:S(2)}, u32[]{:S(2)}) %all-to-all-start.1) | async-done | bytes 288 | tf_op jit(solution)/shard_map/all_to_all | solution.py:27
  100.0 62.2 %all-reduce.12 = f32[256]{0:T(256)S(1)} all-reduce(f32[256]{0:T(256)S(1)} %dynamic-update-slice.12), channel_id=15, replica_groups=mesh['dp_0'=4,'dp_1'=8,'seq_0'=4,'seq_1'=2] {'dp_0','dp_1'}, use_global_device_ids=true, to_apply=%add.12 | all-reduce | flops 256 | bytes 2048
  162.3 4.8 %all-gather.17.cloned.1.call-done = f32[16384,64]{0,1:T(8,128)} async-done(((f32[512,64]{0,1:T(8,128)}), f32[16384,64]{0,1:T(8,128)}) %all-gather.17.cloned.1.call-update) | async-done | bytes 4194320 | tf_op jit(solution)/shard_map/all_gather | solution.py:32
  167.2 4.6 %copy.26 = f32[8,8,32,512]{3,2,1,0:T(8,128)S(1)} copy(f32[8,8,32,512]{3,1,2,0:T(8,128)} %bitcast.33) | data formatting | bytes 8388608
  171.7 0.7 bitcast_reduce_fusion
  172.7 0.5 maximum_dynamic-update-slice_fusion
  173.2 1.0 copy-done.2
  174.3 66.3 %all-reduce.20.cloned.1.call-done = f32[262208]{0:T(1024)} async-done(((f32[262208]{0:T(1024)}), f32[262208]{0:T(1024)}) %all-reduce.20.cloned.1.call-update) | async-done | bytes 1048848
  240.6 1.8 reshape.82
  242.4 1.0 slice.8
  243.4 0.6 reshape.67
  244.0 2.1 reshape_reshape.3
  246.1 1.6 copy.23
  (78 shorter events, 5.0 us)
Async XLA Ops:
  7.2 56.2 %copy-start = (bf16[4096,64]{0,1:T(8,128)(2,1)S(1)}, bf16[4096,64]{0,1:T(8,128)(2,1)}, u32[]{:S(2)}) copy-start(bf16[4096,64]{0,1:T(8,128)(2,1)} %param.7) | copy-start | bytes 1572868
  7.2 160.0 %all-gather.17.cloned.1.call-start = ((), (), s32[]{:S(2)}) async-start(), calls=%async_computation.2 | async-start | bytes 4325376 | tf_op jit(solution)/shard_map/all_gather | solution.py:32
  63.3 6.3 %copy-start.4 = (f32[1024]{0:T(1024)}, f32[1024]{0:T(1024)S(1)}, u32[]{:S(2)}) copy-start(f32[1024]{0:T(1024)S(1)} %select_reduce_fusion.2) | copy-start | bytes 12292
  63.3 6.3 %copy-start.1 = (bf16[1,1024,4096]{2,1,0:T(8,128)(2,1)S(1)}, bf16[1,1024,4096]{2,1,0:T(8,128)(2,1)}, u32[]{:S(2)}) copy-start(bf16[1,1024,4096]{2,1,0:T(8,128)(2,1)} %param.6) | copy-start | bytes 25165828
  63.4 6.3 %copy-start.3 = (s32[1,1024]{1,0:T(1,128)S(1)}, s32[1,1024]{1,0:T(1,128)}, u32[]{:S(2)}) copy-start(s32[1,1024]{1,0:T(1,128)} %param.10) | copy-start | bytes 12292
  71.2 23.4 %copy-start.6 = (u32[256]{0:T(256)S(1)}, u32[256]{0:T(256)}, u32[]{:S(2)}) copy-start(u32[256]{0:T(256)} %constant.87) | copy-start | bytes 3076
  71.2 24.0 %copy-start.5 = (u32[256]{0:T(256)S(1)}, u32[256]{0:T(256)}, u32[]{:S(2)}) copy-start(u32[256]{0:T(256)} %constant.82) | copy-start | bytes 3076
  91.3 8.5 %all-to-all-start.1 = ((f32[8,1,8]{2,1,0:T(1,128)}), f32[8,1,8]{2,1,0:T(1,128)S(1)}, u32[]{:S(2)}, u32[]{:S(2)}) async-start(f32[8,1,8]{2,1,0:T(1,128)} %bitcast.10), calls=%async_computation.1 | async-start | bytes 8192 | tf_op jit(solution)/shard_map/all_to_all | solution.py:27
  94.5 146.0 %all-reduce.20.cloned.1.call-start = ((), (), s32[]{:S(2)}) async-start(), calls=%async_computation.3 | async-start | bytes 2105344
  173.2 1.0 copy-start.2
Sparse Core Ops, SparseCore 0:
  90.6 76.5 all-gather.16
  174.4 66.0 all-reduce.19
